TPU v7x, 32 devices: a whole 2x2x4 slice. The times are simulated.
32 devices in a mesh: space: 4 (over y, x), sub: 8 (over z, core).
Axes of the slice: x: 2, y: 2, z: 4, core: 2. Of those that a mesh axis runs over, the one named last changes fastest.
Arguments:
- positions: float32 [3, 4, 512, 128], P(None, 'space', 'sub'), may hold values from 0 to 1.5
- masses: float32 [4, 512, 128], P('space', 'sub'), may hold values from 0.1 to 1
- occupancy: int32 [4, 512], P('space', 'sub'), may hold values from 1 to 128
- export_slots: int32 [4, 256], P('space', 'sub'), may hold values from 0 to 63, as said below
- export_count: int32 [4, 8], P('space', 'sub'), may hold values from 16 to 32
- pair_list: int32 [2, 4, 512], P(None, 'space', 'sub'), may hold values from 0 to 319, as said below
- pair_count: int32 [4, 8], P('space', 'sub'), may hold values from 16 to 64
Outputs:
- forces: float32 [3, 4, 512, 128], P(None, 'space', 'sub')
Inputs may be any that keep to these rules, and one draw needn't show every extreme that they name: `export_slots`: the 32 entries of one device are distinct own-leaf indices. `pair_list`: row 0 is a target own leaf, below 64; row 1 is a source pool leaf, below 320, never equal to the target.
All inputs are finite; a program needn't handle non-finite values.
Results may differ from a plain program's by a relative error of at most 0.0003.
Values sent between devices are 32-bit elements; how exact they have to be, the bound alone decides.
A program may use at most 64 MiB of HBM per device.

v0:
```python
import functools

import jax
import jax.numpy as jnp
from jax import lax
from jax.experimental import pallas as pl
from jax.experimental.pallas import tpu as pltpu
from jax.sharding import PartitionSpec as P

OFFSETS = ((-1, -1), (-1, 0), (-1, 1), (0, -1), (0, 1), (1, -1), (1, 0), (1, 1))
SOFTEN = 0.05
CENTRE = 0.75
MESH = pl.DeviceIdType.MESH
F32, BF16 = jnp.float32, jnp.bfloat16
UNROLL = 16
CHUNKS = 1
CUTS = (12, 16)
PAIR_CUTS = (4, 8, 12, 16)


def split3(v):
    high = v.astype(BF16).astype(F32)
    rest = v - high
    mid = rest.astype(BF16).astype(F32)
    return high, mid, rest - mid


def rows_of(sub, values):
    out = jnp.zeros(sub.shape, F32)
    for index, value in enumerate(values):
        out = jnp.where(sub == index, value, out)
    return out


def kernel(pos_in, mass_in, occ_in, slots_in, count_in, pairs_in, live_in, out,
           pos, mass, occ, occ_s, slots_v, slots_s, count_s, pairs_v, pairs_s, live_s,
           pool, export, turned, kept, self_res, tgt_res, src_res, ghost, came, crossing, crossed,
           load_sem, send_sem, recv_sem, back_send, back_recv):
    leaves, width = mass.shape[1:]
    sent = slots_s.shape[1]
    pairs = pairs_s.shape[2]
    block_rows = 4 * sent
    own_blocks = leaves // sent
    n_space, n_sub = lax.axis_size("space"), lax.axis_size("sub")
    s, r = lax.axis_index("space"), lax.axis_index("sub")
    device = {
        (-1, 0): (lax.rem(s + n_space - 1, n_space), r),
        (1, 0): (lax.rem(s + 1, n_space), r),
        (0, -1): (s, lax.rem(r + n_sub - 1, n_sub)),
        (0, 1): (s, lax.rem(r + 1, n_sub)),
    }
    barrier = pltpu.get_barrier_semaphore()
    for where in device.values():
        pl.semaphore_signal(barrier, inc=1, device_id=where, device_id_type=MESH)
    loads = [
        pltpu.make_async_copy(source, target, load_sem.at[index])
        for index, (source, target) in enumerate((
            (slots_in, slots_s), (occ_in, occ_s), (count_in, count_s), (pos_in, pos),
            (mass_in, mass), (occ_in, occ), (slots_in, slots_v), (pairs_in, pairs_v),
            (pairs_in, pairs_s), (live_in, live_s),
        ))
    ]
    for copy in loads:
        copy.start()
    for copy in loads[:5]:
        copy.wait()

    def row(leaf, c):
        return lax.div(leaf, sent) * block_rows + lax.rem(leaf, sent) + c * sent

    def load(leaf):
        start = row(leaf, 0)
        return [pool[pl.ds(start + c * sent, 1), :] for c in range(4)]

    lane_row = lax.broadcasted_iota(jnp.int32, (1, width), 1)
    for g in range(sent):
        slot = slots_s[0, g]
        filled = jnp.where(g < count_s[0, 0], occ_s[0, slot], 0)
        for c in range(3):
            export[pl.ds(c * sent + g, 1), :] = pos[c, 0, pl.ds(slot, 1), :] - CENTRE
        export[pl.ds(3 * sent + g, 1), :] = jnp.where(
            lane_row < filled, mass[0, pl.ds(slot, 1), :], 0.0
        )

    sub = lax.broadcasted_iota(jnp.int32, (8, width), 0)
    low = sub < 4

    chunk_rows = block_rows // CHUNKS
    direct = ((-1, 0), (1, 0), (0, -1), (0, 1))

    def send(source, towards, arrives, chunk):
        index = OFFSETS.index(arrives)
        start = (own_blocks + index) * block_rows + chunk * chunk_rows
        return pltpu.make_async_remote_copy(
            src_ref=source, dst_ref=pool.at[pl.ds(start, chunk_rows), :],
            send_sem=send_sem.at[index, chunk], recv_sem=recv_sem.at[index, chunk],
            device_id=device[towards], device_id_type=MESH,
        )

    copies = {}
    for chunk in range(CHUNKS):
        for a, b in direct:
            source = export.at[pl.ds(chunk * chunk_rows, chunk_rows), :]
            copies[(a, b, chunk)] = send(source, (-a, -b), (a, b), chunk)
        for a in (-1, 1):
            start = (own_blocks + OFFSETS.index((a, 0))) * block_rows + chunk * chunk_rows
            for b in (-1, 1):
                source = pool.at[pl.ds(start, chunk_rows), :]
                copies[(a, b, chunk)] = send(source, (0, -b), (a, b), chunk)

    pl.semaphore_wait(barrier, 4)
    for near in (direct[:2], direct[2:]):
        for chunk in range(CHUNKS):
            for a, b in near:
                copies[(a, b, chunk)].start()

    for copy in loads[5:]:
        copy.wait()
    eye = (
        lax.broadcasted_iota(jnp.int32, (leaves, leaves), 0)
        == lax.broadcasted_iota(jnp.int32, (leaves, leaves), 1)
    )
    occ_col = jnp.sum(jnp.where(eye, occ[...].astype(F32), 0.0), axis=1, keepdims=True)
    lane = lax.broadcasted_iota(jnp.int32, (leaves, width), 1).astype(F32)
    own_mass = jnp.where(lane < occ_col, mass[0], 0.0)
    for block in range(own_blocks):
        part = slice(block * sent, (block + 1) * sent)
        for c in range(3):
            pool[pl.ds(block * block_rows + c * sent, sent), :] = pos[c, 0, part] - CENTRE
        pool[pl.ds(block * block_rows + 3 * sent, sent), :] = own_mass[part]

    def features(x, y, z):
        q = x * x + y * y + z * z
        return rows_of(sub, (x, y, z, 1.0, q + SOFTEN)), q

    def right_operand(vb):
        h, m, l = split3(vb)
        return jnp.concatenate([h, m, h, l, h, m], axis=0).astype(BF16)

    def left_operand(vb, q):
        va = jnp.where(sub < 3, -2.0 * vb, rows_of(sub, (0.0, 0.0, 0.0, q, 1.0)))
        h, m, l = split3(va)
        return jnp.concatenate([h, h, m, h, l, m], axis=0)

    def force_operand(vb, m):
        moment = m * rows_of(sub, (vb[0:1], vb[1:2], vb[2:3], 1.0, vb[0:1], vb[1:2], vb[2:3], 1.0))
        h, mid, l = split3(moment)
        both = jnp.concatenate([jnp.where(low, h, mid), jnp.where(low, l, 0.0)], axis=0).astype(BF16)
        return jnp.concatenate([both, both], axis=1)

    def weights(left, right):
        soft = jnp.dot(left, right, preferred_element_type=F32)
        fall = jnp.maximum((1.0 + SOFTEN) - soft, 0.0)
        root = lax.rsqrt(soft)
        part = fall * root
        weight = part * part * root
        high = weight.astype(BF16)
        rest = (weight - high.astype(F32)).astype(BF16)
        return high, rest

    def finish(product, vb, m):
        total = product[:8] + pltpu.roll(product[:8], 4, 0) + product[8:]
        return m * (total - vb * total[3:4])

    def self_pair(leaf):
        x, y, z, m = load(leaf)
        vb, q = features(x, y, z)
        left = jnp.transpose(left_operand(vb, q)).astype(BF16)
        turned[leaf] = left
        high, rest = weights(left, right_operand(vb))
        product = jnp.dot(
            force_operand(vb, m), jnp.concatenate([high, rest], axis=0), preferred_element_type=F32
        )
        self_res[pl.ds(pl.multiple_of(leaf * 8, 8), 8), :] = finish(product, vb, m)

    def listed_pair(p):
        target, source = pairs_s[0, 0, p], pairs_s[1, 0, p]
        x, y, z, m_t = load(target)
        vb_t, _ = features(x, y, z)
        x, y, z, m_u = load(source)
        vb_u, _ = features(x, y, z)
        high, rest = weights(turned[target], right_operand(vb_u))
        onto_source = jnp.dot(
            force_operand(vb_t, m_t), jnp.concatenate([high, rest], axis=0),
            preferred_element_type=F32,
        )
        kept[p, :, :width] = high
        kept[p, :, width:] = rest
        src_res[pl.ds(pl.multiple_of(p * 8, 8), 8), :] = finish(onto_source, vb_u, m_u)

    def target_side(p):
        target, source = pairs_s[0, 0, p], pairs_s[1, 0, p]
        x, y, z, m_t = load(target)
        vb_t, _ = features(x, y, z)
        x, y, z, m_u = load(source)
        vb_u, _ = features(x, y, z)
        onto_target = lax.dot_general(
            force_operand(vb_u, m_u), kept[p], (((1,), (1,)), ((), ())),
            preferred_element_type=F32,
        )
        tgt_res[pl.ds(pl.multiple_of(p * 8, 8), 8), :] = finish(onto_target, vb_t, m_t)

    def run(body, first, last):
        def step(i, carry):
            for j in range(UNROLL):
                body(first + i * UNROLL + j)
            return carry

        lax.fori_loop(0, (last - first) // UNROLL, step, 0)

    cuts = [leaves * cut // 16 for cut in CUTS]
    run(self_pair, 0, cuts[0])
    for chunk in range(CHUNKS):
        for a in (-1, 1):
            copies[(a, 0, chunk)].wait_recv()
            for b in (-1, 1):
                copies[(a, b, chunk)].start()
        run(self_pair, cuts[chunk], cuts[chunk + 1])
    for chunk in range(CHUNKS):
        for a, b in OFFSETS:
            if b != 0:
                copies[(a, b, chunk)].wait_recv()
    run(listed_pair, 0, pairs)

    def component(ref, c, count):
        return ref[pl.ds(c, count, stride=8), :]

    def stacked(values):
        return jnp.concatenate([part for part in split3(values)], axis=0).astype(BF16)

    pair_live = lax.broadcasted_iota(jnp.int32, (1, pairs), 1) < live_s[0, 0]

    def onehot(rows, start, wanted, live):
        which = lax.broadcasted_iota(jnp.int32, (rows, wanted.shape[1]), 0) + start
        hit = which == wanted
        if live is not None:
            hit = jnp.logical_and(hit, live)
        hit = jnp.where(hit, 1.0, 0.0)
        return hit

    tgt_row, src_row = pairs_v[0], pairs_v[1]
    src_parts = [stacked(component(src_res, c, pairs)) for c in range(3)]
    src_all = jnp.concatenate(src_parts, axis=1)
    hit = onehot(8 * sent, leaves, src_row, pair_live)
    onto_ghost = jnp.concatenate([hit, hit, hit], axis=1).astype(BF16)
    ghost_force = jnp.dot(onto_ghost, src_all, preferred_element_type=F32)
    for k in range(8):
        for c in range(3):
            ghost[k, pl.ds(c * sent, sent), :] = ghost_force[
                k * sent:(k + 1) * sent, c * width:(c + 1) * width
            ]

    def give(source, target, towards, index, c):
        return pltpu.make_async_remote_copy(
            src_ref=source, dst_ref=target,
            send_sem=back_send.at[index, c], recv_sem=back_recv.at[index, c],
            device_id=device[towards], device_id_type=MESH,
        )

    def part(c):
        return pl.ds(c * sent, sent)

    back = {}
    for near in ((-1, 1), (0,)):
        for c in range(3):
            for a in near:
                for b in (-1, 1):
                    slot = (a + 1) * 2 + (b + 1) // 2
                    back[(a, b, c)] = give(
                        ghost.at[OFFSETS.index((a, b)), part(c), :], came.at[slot, part(c), :],
                        (0, b), slot, c,
                    )
                    back[(a, b, c)].start()

    def arrived(a, c):
        first = (a + 1) * 2
        return came[first, part(c), :] + came[first + 1, part(c), :]

    pair_cuts = [pairs * cut // 16 for cut in PAIR_CUTS]
    run(target_side, 0, pair_cuts[0])
    for c in range(3):
        for a in (-1, 1):
            side = (a + 1) // 2
            for b in (-1, 1):
                back[(a, b, c)].wait_recv()
            crossing[side, part(c), :] = ghost[OFFSETS.index((a, 0)), part(c), :] + arrived(a, c)
            back[(a, 0, c)] = give(
                crossing.at[side, part(c), :], crossed.at[side, part(c), :], (a, 0), 6 + side, c
            )
            back[(a, 0, c)].start()
        run(target_side, pair_cuts[c], pair_cuts[c + 1])
    tgt_all = jnp.concatenate([stacked(component(tgt_res, c, pairs)) for c in range(3)], axis=1)
    hit_t = onehot(leaves, 0, tgt_row, pair_live)
    hit_s = onehot(leaves, 0, src_row, pair_live)
    own_force = jnp.dot(
        jnp.concatenate([hit_t, hit_t, hit_t, hit_s, hit_s, hit_s], axis=1).astype(BF16),
        jnp.concatenate([tgt_all, src_all], axis=0), preferred_element_type=F32,
    )

    returned = []
    for c in range(3):
        for b in (-1, 1):
            back[(0, b, c)].wait_recv()
        for a in (-1, 1):
            back[(a, 0, c)].wait_recv()
        returned.append(stacked(arrived(0, c) + crossed[0, part(c), :] + crossed[1, part(c), :]))
    parts = jnp.concatenate(returned, axis=1)
    hit = onehot(leaves, 0, slots_v[...], None)
    own_force = own_force + jnp.dot(
        jnp.concatenate([hit, hit, hit], axis=1).astype(BF16), parts, preferred_element_type=F32
    )
    for c in range(3):
        out[c, 0] = component(self_res, c, leaves) + own_force[:, c * width:(c + 1) * width]
    for copy in (*copies.values(), *back.values()):
        copy.wait_send()


def local(positions, masses, occupancy, export_slots, export_count, pair_list, pair_count):
    leaves, width = masses.shape[1:]
    sent = export_slots.shape[1]
    pairs = pair_list.shape[2]
    return pl.pallas_call(
        kernel,
        out_shape=pltpu.VMEM(positions.shape, F32),
        in_specs=[pl.BlockSpec(memory_space=pl.ANY)] * 7,
        out_specs=pl.BlockSpec(memory_space=pltpu.VMEM),
        scratch_shapes=[
            pltpu.VMEM(positions.shape, F32),
            pltpu.VMEM(masses.shape, F32),
            pltpu.VMEM(occupancy.shape, jnp.int32),
            pltpu.SMEM(occupancy.shape, jnp.int32),
            pltpu.VMEM(export_slots.shape, jnp.int32),
            pltpu.SMEM(export_slots.shape, jnp.int32),
            pltpu.SMEM(export_count.shape, jnp.int32),
            pltpu.VMEM(pair_list.shape, jnp.int32),
            pltpu.SMEM(pair_list.shape, jnp.int32),
            pltpu.SMEM(pair_count.shape, jnp.int32),
            pltpu.VMEM((4 * (leaves + 8 * sent), width), F32),
            pltpu.VMEM((4 * sent, width), F32),
            pltpu.VMEM((leaves, width, 48), BF16),
            pltpu.VMEM((pairs, width, 2 * width), BF16),
            pltpu.VMEM((8 * leaves, width), F32),
            pltpu.VMEM((8 * pairs, width), F32),
            pltpu.VMEM((8 * pairs, width), F32),
            pltpu.VMEM((8, 3 * sent, width), F32),
            pltpu.VMEM((6, 3 * sent, width), F32),
            pltpu.VMEM((2, 3 * sent, width), F32),
            pltpu.VMEM((2, 3 * sent, width), F32),
            pltpu.SemaphoreType.DMA((10,)),
            pltpu.SemaphoreType.DMA((8, CHUNKS)),
            pltpu.SemaphoreType.DMA((8, CHUNKS)),
            pltpu.SemaphoreType.DMA((8, 3)),
            pltpu.SemaphoreType.DMA((8, 3)),
        ],
        compiler_params=pltpu.CompilerParams(collective_id=0, has_side_effects=True),
    )(positions, masses, occupancy, export_slots, export_count, pair_list, pair_count)


def solution(mesh):
    return jax.shard_map(
        local,
        mesh=mesh,
        in_specs=(
            P(None, "space", "sub", None),
            P("space", "sub", None),
            P("space", "sub"),
            P("space", "sub"),
            P("space", "sub"),
            P(None, "space", "sub"),
            P("space", "sub"),
        ),
        out_specs=P(None, "space", "sub", None),
        check_vma=False,
    )
```

profile of v0, /device:TPU:0, one launch (start us, length us, event | category | flops | bytes accessed | tf_op | source)
XLA Modules:
  0.0 26.9 jit_solution(13816472491220305372)
XLA Ops:
  1.3 25.0 %shard_map.73 = f32[3,1,64,128]{3,2,1,0:T(8,128)S(1)} custom-call(f32[3,1,64,128]{3,2,1,0:T(8,128)} %pos_in.1, f32[1,64,128]{2,1,0:T(8,128)} %mass_in.1, s32[1,64]{1,0:T(1,128)} %occ_in.1, s32[1,32]{1,0:T(1,128)} %slots_in.1, s32[1,1]{1,0:T(1,128)S(6)} %copy.10.count_in, s32[2,1,64]{2,1,0:T(1,128)} %pairs_in.1, s32[1,1]{1,0:T(1,128)S(6)} %copy.11.live_in), custom_call_target="tpu_custom_call" | custom-call | tf_op jit(solution)/shard_map/pallas_call | solution.py:322
  26.3 0.6 %copy.9 = f32[3,1,64,128]{3,2,1,0:T(8,128)} copy(f32[3,1,64,128]{3,2,1,0:T(8,128)S(1)} %shard_map.73) | data formatting | bytes 196608
where the time goes:
time: 27.1 us; the launch traced here: 26.9 us
  Pallas kernels  25 us (92%)
  between operations  1.3 us (5%)
  local copies, waits for them, and re-layouts  0.64 us (2%)
    pallas_call x1, Pallas kernels, local(): pl.pallas_call(kernel, out_shape=pltpu.VMEM(positions.shape, F32), in_spe...  25 us
    unnamed x1, local copies, waits for them, and re-layouts  0.64 us

commit v1 on v0

--- a/solution.py
+++ b/solution.py
@@ -34,8 +34,8 @@
 
 def kernel(pos_in, mass_in, occ_in, slots_in, count_in, pairs_in, live_in, out,
            pos, mass, occ, occ_s, slots_v, slots_s, count_s, pairs_v, pairs_s, live_s,
-           pool, export, turned, kept, self_res, tgt_res, src_res, ghost, came, crossing, crossed,
-           load_sem, send_sem, recv_sem, back_send, back_recv):
+           pool, export, turned, kept, self_res, tgt_res, src_res, ghost, came, crossing,
+           load_sem, send_sem, recv_sem, back_recv):
     leaves, width = mass.shape[1:]
     sent = slots_s.shape[1]
     pairs = pairs_s.shape[2]
@@ -93,8 +93,14 @@
         start = (own_blocks + index) * block_rows + chunk * chunk_rows
         return pltpu.make_async_remote_copy(
             src_ref=source, dst_ref=pool.at[pl.ds(start, chunk_rows), :],
-            send_sem=send_sem.at[index, chunk], recv_sem=recv_sem.at[index, chunk],
+            send_sem=send_sem.at[0], recv_sem=recv_sem.at[2 if arrives[1] else (arrives[0] + 1) // 2, chunk],
             device_id=device[towards], device_id_type=MESH,
+        )
+
+    def whole(ref, sem):
+        return pltpu.make_async_remote_copy(
+            src_ref=ref, dst_ref=ref, send_sem=sem, recv_sem=sem,
+            device_id=device[(0, 1)], device_id_type=MESH,
         )
 
     copies = {}
@@ -217,9 +223,8 @@
                 copies[(a, b, chunk)].start()
         run(self_pair, cuts[chunk], cuts[chunk + 1])
     for chunk in range(CHUNKS):
-        for a, b in OFFSETS:
-            if b != 0:
-                copies[(a, b, chunk)].wait_recv()
+        sub_rows = pl.ds(own_blocks * block_rows, 6 * chunk_rows)
+        whole(pool.at[sub_rows, :], recv_sem.at[2, chunk]).wait_recv()
     run(listed_pair, 0, pairs)
 
     def component(ref, c, count):
@@ -250,10 +255,10 @@
                 k * sent:(k + 1) * sent, c * width:(c + 1) * width
             ]
 
-    def give(source, target, towards, index, c):
+    def give(source, slot, towards, c):
         return pltpu.make_async_remote_copy(
-            src_ref=source, dst_ref=target,
-            send_sem=back_send.at[index, c], recv_sem=back_recv.at[index, c],
+            src_ref=source, dst_ref=came.at[c, slot],
+            send_sem=send_sem.at[1], recv_sem=back_recv.at[slot // 4, c],
             device_id=device[towards], device_id_type=MESH,
         )
 
@@ -265,27 +270,25 @@
         for c in range(3):
             for a in near:
                 for b in (-1, 1):
-                    slot = (a + 1) * 2 + (b + 1) // 2
+                    slot = {-1: 0, 1: 2, 0: 4}[a] + (b + 1) // 2
                     back[(a, b, c)] = give(
-                        ghost.at[OFFSETS.index((a, b)), part(c), :], came.at[slot, part(c), :],
-                        (0, b), slot, c,
+                        ghost.at[OFFSETS.index((a, b)), part(c), :], slot, (0, b), c
                     )
                     back[(a, b, c)].start()
 
     def arrived(a, c):
-        first = (a + 1) * 2
-        return came[first, part(c), :] + came[first + 1, part(c), :]
+        first = {-1: 0, 1: 2, 0: 4}[a]
+        return came[c, first] + came[c, first + 1]
 
     pair_cuts = [pairs * cut // 16 for cut in PAIR_CUTS]
     run(target_side, 0, pair_cuts[0])
     for c in range(3):
+        whole(came.at[c, pl.ds(0, 4)], back_recv.at[0, c]).wait_recv()
         for a in (-1, 1):
             side = (a + 1) // 2
-            for b in (-1, 1):
-                back[(a, b, c)].wait_recv()
             crossing[side, part(c), :] = ghost[OFFSETS.index((a, 0)), part(c), :] + arrived(a, c)
             back[(a, 0, c)] = give(
-                crossing.at[side, part(c), :], crossed.at[side, part(c), :], (a, 0), 6 + side, c
+                crossing.at[side, part(c), :], 6 + side, (a, 0), c
             )
             back[(a, 0, c)].start()
         run(target_side, pair_cuts[c], pair_cuts[c + 1])
@@ -299,11 +302,8 @@
 
     returned = []
     for c in range(3):
-        for b in (-1, 1):
-            back[(0, b, c)].wait_recv()
-        for a in (-1, 1):
-            back[(a, 0, c)].wait_recv()
-        returned.append(stacked(arrived(0, c) + crossed[0, part(c), :] + crossed[1, part(c), :]))
+        whole(came.at[c, pl.ds(4, 4)], back_recv.at[1, c]).wait_recv()
+        returned.append(stacked(arrived(0, c) + came[c, 6] + came[c, 7]))
     parts = jnp.concatenate(returned, axis=1)
     hit = onehot(leaves, 0, slots_v[...], None)
     own_force = own_force + jnp.dot(
@@ -311,8 +311,8 @@
     )
     for c in range(3):
         out[c, 0] = component(self_res, c, leaves) + own_force[:, c * width:(c + 1) * width]
-    for copy in (*copies.values(), *back.values()):
-        copy.wait_send()
+    whole(pool.at[pl.ds(own_blocks * block_rows, 8 * block_rows), :], send_sem.at[0]).wait_send()
+    whole(ghost, send_sem.at[1]).wait_send()
 
 
 def local(positions, masses, occupancy, export_slots, export_count, pair_list, pair_count):
@@ -343,14 +343,12 @@
             pltpu.VMEM((8 * pairs, width), F32),
             pltpu.VMEM((8 * pairs, width), F32),
             pltpu.VMEM((8, 3 * sent, width), F32),
-            pltpu.VMEM((6, 3 * sent, width), F32),
-            pltpu.VMEM((2, 3 * sent, width), F32),
+            pltpu.VMEM((3, 8, sent, width), F32),
             pltpu.VMEM((2, 3 * sent, width), F32),
             pltpu.SemaphoreType.DMA((10,)),
-            pltpu.SemaphoreType.DMA((8, CHUNKS)),
-            pltpu.SemaphoreType.DMA((8, CHUNKS)),
-            pltpu.SemaphoreType.DMA((8, 3)),
-            pltpu.SemaphoreType.DMA((8, 3)),
+            pltpu.SemaphoreType.DMA((2,)),
+            pltpu.SemaphoreType.DMA((3, CHUNKS)),
+            pltpu.SemaphoreType.DMA((2, 3)),
         ],
         compiler_params=pltpu.CompilerParams(collective_id=0, has_side_effects=True),
     )(positions, masses, occupancy, export_slots, export_count, pair_list, pair_count)

time: 27.1 us -> 26.9 us (level)
  no operation moved by 1% of the time
where the time goes in v1:
time: 26.9 us; the launch traced here: 26.7 us
  Pallas kernels  24.8 us (92%)
  between operations  1.3 us (5%)
  local copies, waits for them, and re-layouts  0.64 us (2%)
    pallas_call x1, Pallas kernels, local(): pl.pallas_call(kernel, out_shape=pltpu.VMEM(positions.shape, F32), in_spe...  24.8 us
    unnamed x1, local copies, waits for them, and re-layouts  0.64 us

profile of v1, /device:TPU:0, one launch (start us, length us, event | category | flops | bytes accessed | tf_op | source)
XLA Modules:
  0.0 26.7 jit_solution(3486812554667905608)
XLA Ops:
  1.3 24.8 %shard_map.73 = f32[3,1,64,128]{3,2,1,0:T(8,128)S(1)} custom-call(f32[3,1,64,128]{3,2,1,0:T(8,128)} %pos_in.1, f32[1,64,128]{2,1,0:T(8,128)} %mass_in.1, s32[1,64]{1,0:T(1,128)} %occ_in.1, s32[1,32]{1,0:T(1,128)} %slots_in.1, s32[1,1]{1,0:T(1,128)S(6)} %copy.10.count_in, s32[2,1,64]{2,1,0:T(1,128)} %pairs_in.1, s32[1,1]{1,0:T(1,128)S(6)} %copy.11.live_in), custom_call_target="tpu_custom_call" | custom-call | tf_op jit(solution)/shard_map/pallas_call | solution.py:322
  26.1 0.6 %copy.9 = f32[3,1,64,128]{3,2,1,0:T(8,128)} copy(f32[3,1,64,128]{3,2,1,0:T(8,128)S(1)} %shard_map.73) | data formatting | bytes 196608

commit v2 on v1

--- a/solution.py
+++ b/solution.py
@@ -13,9 +13,8 @@
 MESH = pl.DeviceIdType.MESH
 F32, BF16 = jnp.float32, jnp.bfloat16
 UNROLL = 16
-CHUNKS = 1
-CUTS = (12, 16)
-PAIR_CUTS = (4, 8, 12, 16)
+CHUNKS = 2
+CUTS = (12, 16, 16)
 
 
 def split3(v):
@@ -44,14 +43,23 @@
     n_space, n_sub = lax.axis_size("space"), lax.axis_size("sub")
     s, r = lax.axis_index("space"), lax.axis_index("sub")
     device = {
-        (-1, 0): (lax.rem(s + n_space - 1, n_space), r),
-        (1, 0): (lax.rem(s + 1, n_space), r),
-        (0, -1): (s, lax.rem(r + n_sub - 1, n_sub)),
-        (0, 1): (s, lax.rem(r + 1, n_sub)),
+        (a, b): (lax.rem(s + n_space + a, n_space), lax.rem(r + n_sub + b, n_sub))
+        for a, b in OFFSETS
     }
+    wraps = {-1: r == 0, 1: r == n_sub - 1}
+    edge = jnp.logical_or(wraps[-1], wraps[1])
     barrier = pltpu.get_barrier_semaphore()
-    for where in device.values():
+
+    def greet(where):
         pl.semaphore_signal(barrier, inc=1, device_id=where, device_id_type=MESH)
+
+    @pl.when(wraps[-1])
+    def _():
+        for a in (-1, 1):
+            greet(device[(a, -1)])
+
+    for where in ((0, -1), (0, 1), (-1, 0), (1, 0)):
+        greet(device[where])
     loads = [
         pltpu.make_async_copy(source, target, load_sem.at[index])
         for index, (source, target) in enumerate((
@@ -86,15 +94,17 @@
     low = sub < 4
 
     chunk_rows = block_rows // CHUNKS
-    direct = ((-1, 0), (1, 0), (0, -1), (0, 1))
-
-    def send(source, towards, arrives, chunk):
-        index = OFFSETS.index(arrives)
-        start = (own_blocks + index) * block_rows + chunk * chunk_rows
+
+    def rows_at(index, chunk=None):
+        start = (own_blocks + OFFSETS.index(index)) * block_rows
+        if chunk is None:
+            return pl.ds(start, block_rows)
+        return pl.ds(start + chunk * chunk_rows, chunk_rows)
+
+    def send(source, where, target, sem, sent_sem=0):
         return pltpu.make_async_remote_copy(
-            src_ref=source, dst_ref=pool.at[pl.ds(start, chunk_rows), :],
-            send_sem=send_sem.at[0], recv_sem=recv_sem.at[2 if arrives[1] else (arrives[0] + 1) // 2, chunk],
-            device_id=device[towards], device_id_type=MESH,
+            src_ref=source, dst_ref=pool.at[target, :], send_sem=send_sem.at[sent_sem],
+            recv_sem=recv_sem.at[sem], device_id=device[where], device_id_type=MESH,
         )
 
     def whole(ref, sem):
@@ -103,23 +113,29 @@
             device_id=device[(0, 1)], device_id_type=MESH,
         )
 
-    copies = {}
-    for chunk in range(CHUNKS):
-        for a, b in direct:
-            source = export.at[pl.ds(chunk * chunk_rows, chunk_rows), :]
-            copies[(a, b, chunk)] = send(source, (-a, -b), (a, b), chunk)
-        for a in (-1, 1):
-            start = (own_blocks + OFFSETS.index((a, 0))) * block_rows + chunk * chunk_rows
-            for b in (-1, 1):
-                source = pool.at[pl.ds(start, chunk_rows), :]
-                copies[(a, b, chunk)] = send(source, (0, -b), (a, b), chunk)
-
-    pl.semaphore_wait(barrier, 4)
-    for near in (direct[:2], direct[2:]):
-        for chunk in range(CHUNKS):
-            for a, b in near:
-                copies[(a, b, chunk)].start()
-
+    rest = 2 * CHUNKS
+    across = {
+        (a, chunk): send(
+            export.at[pl.ds(chunk * chunk_rows, chunk_rows), :], (-a, 0),
+            rows_at((a, 0), chunk), 2 * chunk + (a + 1) // 2,
+        )
+        for chunk in range(CHUNKS) for a in (-1, 1)
+    }
+
+    def forward(a, b, chunk):
+        rows = rows_at((a, 0), chunk)
+        return send(pool.at[rows, :], (0, -b), rows_at((a, b), chunk), rest)
+
+    pl.semaphore_wait(barrier, jnp.where(wraps[1], 6, 4))
+    @pl.when(wraps[1])
+    def _():
+        for a in (-1, 1):
+            send(export, (-a, 1), rows_at((a, -1)), rest).start()
+
+    for copy in across.values():
+        copy.start()
+    for b in (-1, 1):
+        send(export, (0, -b), rows_at((0, b)), rest + (b + 1) // 2).start()
     for copy in loads[5:]:
         copy.wait()
     eye = (
@@ -206,26 +222,34 @@
         )
         tgt_res[pl.ds(pl.multiple_of(p * 8, 8), 8), :] = finish(onto_target, vb_t, m_t)
 
-    def run(body, first, last):
+    def run(body, first, last, unroll=UNROLL):
         def step(i, carry):
-            for j in range(UNROLL):
-                body(first + i * UNROLL + j)
+            for j in range(unroll):
+                body(first + i * unroll + j)
             return carry
 
-        lax.fori_loop(0, (last - first) // UNROLL, step, 0)
+        lax.fori_loop(0, (last - first) // unroll, step, 0)
 
     cuts = [leaves * cut // 16 for cut in CUTS]
     run(self_pair, 0, cuts[0])
     for chunk in range(CHUNKS):
         for a in (-1, 1):
-            copies[(a, 0, chunk)].wait_recv()
+            across[(a, chunk)].wait_recv()
             for b in (-1, 1):
-                copies[(a, b, chunk)].start()
+                @pl.when(jnp.logical_not(wraps[-b]))
+                def _():
+                    forward(a, b, chunk).start()
         run(self_pair, cuts[chunk], cuts[chunk + 1])
-    for chunk in range(CHUNKS):
-        sub_rows = pl.ds(own_blocks * block_rows, 6 * chunk_rows)
-        whole(pool.at[sub_rows, :], recv_sem.at[2, chunk]).wait_recv()
-    run(listed_pair, 0, pairs)
+    ghosts = own_blocks * block_rows
+    whole(pool.at[rows_at((0, 1)), :], recv_sem.at[rest + 1]).wait_recv()
+
+    @pl.when(wraps[1])
+    def _():
+        for a in (-1, 1):
+            send(pool.at[rows_at((0, 1)), :], (-a, 0), rows_at((a, 1)), rest, 2).start()
+
+    whole(pool.at[pl.ds(ghosts, 5 * block_rows), :], recv_sem.at[rest]).wait_recv()
+    run(listed_pair, 0, pairs, 64)
 
     def component(ref, c, count):
         return ref[pl.ds(c, count, stride=8), :]
@@ -248,50 +272,55 @@
     src_all = jnp.concatenate(src_parts, axis=1)
     hit = onehot(8 * sent, leaves, src_row, pair_live)
     onto_ghost = jnp.concatenate([hit, hit, hit], axis=1).astype(BF16)
-    ghost_force = jnp.dot(onto_ghost, src_all, preferred_element_type=F32)
-    for k in range(8):
-        for c in range(3):
-            ghost[k, pl.ds(c * sent, sent), :] = ghost_force[
-                k * sent:(k + 1) * sent, c * width:(c + 1) * width
-            ]
-
-    def give(source, slot, towards, c):
+
+    def part(c):
+        return pl.ds(c * sent, sent)
+
+    def slot_of(a, b):
+        return {-1: 0, 1: 2, 0: 4}[a] + (b + 1) // 2
+
+    def give(source, slot, where, c, last):
         return pltpu.make_async_remote_copy(
             src_ref=source, dst_ref=came.at[c, slot],
-            send_sem=send_sem.at[1], recv_sem=back_recv.at[slot // 4, c],
-            device_id=device[towards], device_id_type=MESH,
-        )
-
-    def part(c):
-        return pl.ds(c * sent, sent)
-
-    back = {}
-    for near in ((-1, 1), (0,)):
-        for c in range(3):
-            for a in near:
-                for b in (-1, 1):
-                    slot = {-1: 0, 1: 2, 0: 4}[a] + (b + 1) // 2
-                    back[(a, b, c)] = give(
-                        ghost.at[OFFSETS.index((a, b)), part(c), :], slot, (0, b), c
-                    )
-                    back[(a, b, c)].start()
-
-    def arrived(a, c):
-        first = {-1: 0, 1: 2, 0: 4}[a]
-        return came[c, first] + came[c, first + 1]
-
-    pair_cuts = [pairs * cut // 16 for cut in PAIR_CUTS]
-    run(target_side, 0, pair_cuts[0])
+            send_sem=send_sem.at[1], recv_sem=back_recv.at[last, c],
+            device_id=where, device_id_type=MESH,
+        )
+
     for c in range(3):
-        whole(came.at[c, pl.ds(0, 4)], back_recv.at[0, c]).wait_recv()
+        ghost_force = jnp.dot(onto_ghost, src_parts[c], preferred_element_type=F32)
+        for k in range(8):
+            ghost[k, part(c), :] = ghost_force[k * sent:(k + 1) * sent]
+        for a in (-1, 1):
+            for b in (-1, 1):
+                to_space, to_sub = device[(a, b)]
+                give(
+                    ghost.at[OFFSETS.index((a, b)), part(c), :], slot_of(a, b),
+                    (jnp.where(wraps[b], to_space, s), to_sub), c, jnp.where(wraps[b], 1, 0),
+                ).start()
+    for c in range(3):
+        for b in (-1, 1):
+            give(
+                ghost.at[OFFSETS.index((0, b)), part(c), :], slot_of(0, b), device[(0, b)], c, 1
+            ).start()
+
+    def took(c, last, at_edge, inside):
+        for which, count in ((edge, at_edge), (jnp.logical_not(edge), inside)):
+            @pl.when(which)
+            def _():
+                whole(came.at[c, pl.ds(0, count)], back_recv.at[last, c]).wait_recv()
+
+    for c in range(3):
+        took(c, 0, 2, 4)
+
         for a in (-1, 1):
             side = (a + 1) // 2
-            crossing[side, part(c), :] = ghost[OFFSETS.index((a, 0)), part(c), :] + arrived(a, c)
-            back[(a, 0, c)] = give(
-                crossing.at[side, part(c), :], 6 + side, (a, 0), c
+            first = came[c, jnp.where(wraps[1], slot_of(a, 1), slot_of(a, -1))]
+            second = came[c, jnp.where(wraps[-1], slot_of(a, -1), slot_of(a, 1))]
+            crossing[side, part(c), :] = (
+                ghost[OFFSETS.index((a, 0)), part(c), :] + first + jnp.where(edge, 0.0, second)
             )
-            back[(a, 0, c)].start()
-        run(target_side, pair_cuts[c], pair_cuts[c + 1])
+            give(crossing.at[side, part(c), :], 6 + side, device[(a, 0)], c, 1).start()
+    run(target_side, 0, pairs)
     tgt_all = jnp.concatenate([stacked(component(tgt_res, c, pairs)) for c in range(3)], axis=1)
     hit_t = onehot(leaves, 0, tgt_row, pair_live)
     hit_s = onehot(leaves, 0, src_row, pair_live)
@@ -300,18 +329,24 @@
         jnp.concatenate([tgt_all, src_all], axis=0), preferred_element_type=F32,
     )
 
-    returned = []
+    hit = onehot(leaves, 0, slots_v[...], None)
+    onto_own = jnp.concatenate([hit, hit, hit], axis=1).astype(BF16)
+    own_force = [
+        component(self_res, c, leaves) + own_force[:, c * width:(c + 1) * width] for c in range(3)
+    ]
     for c in range(3):
-        whole(came.at[c, pl.ds(4, 4)], back_recv.at[1, c]).wait_recv()
-        returned.append(stacked(arrived(0, c) + came[c, 6] + came[c, 7]))
-    parts = jnp.concatenate(returned, axis=1)
-    hit = onehot(leaves, 0, slots_v[...], None)
-    own_force = own_force + jnp.dot(
-        jnp.concatenate([hit, hit, hit], axis=1).astype(BF16), parts, preferred_element_type=F32
-    )
-    for c in range(3):
-        out[c, 0] = component(self_res, c, leaves) + own_force[:, c * width:(c + 1) * width]
-    whole(pool.at[pl.ds(own_blocks * block_rows, 8 * block_rows), :], send_sem.at[0]).wait_send()
+        took(c, 1, 6, 4)
+
+        far = [came[c, jnp.where(wraps[-1], slot_of(a, 1), slot_of(a, -1))] for a in (-1, 1)]
+        returned = stacked(
+            came[c, 4] + came[c, 5] + came[c, 6] + came[c, 7] + jnp.where(edge, far[0] + far[1], 0.0)
+        )
+        out[c, 0] = own_force[c] + jnp.dot(onto_own, returned, preferred_element_type=F32)
+    for which, sem, count in ((r == 0, 0, 6), (r != 0, 0, 8), (wraps[1], 2, 2)):
+        @pl.when(which)
+        def _():
+            whole(pool.at[pl.ds(ghosts, count * block_rows), :], send_sem.at[sem]).wait_send()
+
     whole(ghost, send_sem.at[1]).wait_send()
 
 
@@ -346,8 +381,8 @@
             pltpu.VMEM((3, 8, sent, width), F32),
             pltpu.VMEM((2, 3 * sent, width), F32),
             pltpu.SemaphoreType.DMA((10,)),
-            pltpu.SemaphoreType.DMA((2,)),
-            pltpu.SemaphoreType.DMA((3, CHUNKS)),
+            pltpu.SemaphoreType.DMA((3,)),
+            pltpu.SemaphoreType.DMA((2 * CHUNKS + 2,)),
             pltpu.SemaphoreType.DMA((2, 3)),
         ],
         compiler_params=pltpu.CompilerParams(collective_id=0, has_side_effects=True),

time: 26.9 us -> 23.5 us (0.87)
  Pallas kernels: 24.8 us -> 21.4 us
    pallas_call x1, Pallas kernels: 24.8 us -> 21.4 us  [local(): pl.pallas_call(kernel, out_shape=pltpu.VMEM(positions.shape, F32), in_spe...]
where the time goes in v2:
time: 23.5 us; the launch traced here: 23.4 us
  Pallas kernels  21.4 us (91%)
  between operations  1.3 us (6%)
  local copies, waits for them, and re-layouts  0.64 us (3%)
    pallas_call x1, Pallas kernels, local(): pl.pallas_call(kernel, out_shape=pltpu.VMEM(positions.shape, F32), in_spe...  21.4 us
    unnamed x1, local copies, waits for them, and re-layouts  0.64 us

profile of v2, /device:TPU:0, one launch (start us, length us, event | category | flops | bytes accessed | tf_op | source)
XLA Modules:
  0.0 23.4 jit_solution(11499959208773318479)
XLA Ops:
  1.3 21.4 %shard_map.73 = f32[3,1,64,128]{3,2,1,0:T(8,128)S(1)} custom-call(f32[3,1,64,128]{3,2,1,0:T(8,128)} %pos_in.1, f32[1,64,128]{2,1,0:T(8,128)} %mass_in.1, s32[1,64]{1,0:T(1,128)} %occ_in.1, s32[1,32]{1,0:T(1,128)} %slots_in.1, s32[1,1]{1,0:T(1,128)S(6)} %copy.10.count_in, s32[2,1,64]{2,1,0:T(1,128)} %pairs_in.1, s32[1,1]{1,0:T(1,128)S(6)} %copy.11.live_in), custom_call_target="tpu_custom_call" | custom-call | tf_op jit(solution)/shard_map/pallas_call | solution.py:357
  22.7 0.6 %copy.9 = f32[3,1,64,128]{3,2,1,0:T(8,128)} copy(f32[3,1,64,128]{3,2,1,0:T(8,128)S(1)} %shard_map.73) | data formatting | bytes 196608

commit v3 on v2

--- a/solution.py
+++ b/solution.py
@@ -33,7 +33,7 @@
 
 def kernel(pos_in, mass_in, occ_in, slots_in, count_in, pairs_in, live_in, out,
            pos, mass, occ, occ_s, slots_v, slots_s, count_s, pairs_v, pairs_s, live_s,
-           pool, export, turned, kept, self_res, tgt_res, src_res, ghost, came, crossing,
+           pool, export, turned, moments, kept, self_res, tgt_res, src_res, ghost, came, crossing, gathered,
            load_sem, send_sem, recv_sem, back_recv):
     leaves, width = mass.shape[1:]
     sent = slots_s.shape[1]
@@ -132,10 +132,10 @@
         for a in (-1, 1):
             send(export, (-a, 1), rows_at((a, -1)), rest).start()
 
+    for b in (1, -1):
+        send(export, (0, -b), rows_at((0, b)), rest + (b + 1) // 2).start()
     for copy in across.values():
         copy.start()
-    for b in (-1, 1):
-        send(export, (0, -b), rows_at((0, b)), rest + (b + 1) // 2).start()
     for copy in loads[5:]:
         copy.wait()
     eye = (
@@ -151,21 +151,27 @@
             pool[pl.ds(block * block_rows + c * sent, sent), :] = pos[c, 0, part] - CENTRE
         pool[pl.ds(block * block_rows + 3 * sent, sent), :] = own_mass[part]
 
-    def features(x, y, z):
-        q = x * x + y * y + z * z
-        return rows_of(sub, (x, y, z, 1.0, q + SOFTEN)), q
+    def load_twice(leaf):
+        start = row(leaf, 0)
+        four = pool[pl.ds(start, 4, stride=sent), :]
+        return jnp.concatenate([four, four], axis=0), pool[pl.ds(start + 3 * sent, 1), :]
+
+    def features(two):
+        return jnp.where(low, jnp.where(sub == 3, 1.0, two), jnp.where(sub == 7, SOFTEN, two * two))
 
     def right_operand(vb):
         h, m, l = split3(vb)
         return jnp.concatenate([h, m, h, l, h, m], axis=0).astype(BF16)
 
-    def left_operand(vb, q):
-        va = jnp.where(sub < 3, -2.0 * vb, rows_of(sub, (0.0, 0.0, 0.0, q, 1.0)))
+    def left_operand(two, q):
+        va = jnp.where(sub < 3, -2.0 * two, jnp.where(sub == 3, q, 1.0))
         h, m, l = split3(va)
         return jnp.concatenate([h, h, m, h, l, m], axis=0)
 
-    def force_operand(vb, m):
-        moment = m * rows_of(sub, (vb[0:1], vb[1:2], vb[2:3], 1.0, vb[0:1], vb[1:2], vb[2:3], 1.0))
+    ones = jnp.logical_or(sub == 3, sub == 7)
+
+    def force_operand(two, m):
+        moment = m * jnp.where(ones, 1.0, two)
         h, mid, l = split3(moment)
         both = jnp.concatenate([jnp.where(low, h, mid), jnp.where(low, l, 0.0)], axis=0).astype(BF16)
         return jnp.concatenate([both, both], axis=1)
@@ -175,10 +181,11 @@
         fall = jnp.maximum((1.0 + SOFTEN) - soft, 0.0)
         root = lax.rsqrt(soft)
         part = fall * root
-        weight = part * part * root
+        return part * part * root
+
+    def halves(weight):
         high = weight.astype(BF16)
-        rest = (weight - high.astype(F32)).astype(BF16)
-        return high, rest
+        return high, (weight - high.astype(F32)).astype(BF16)
 
     def finish(product, vb, m):
         total = product[:8] + pltpu.roll(product[:8], 4, 0) + product[8:]
@@ -186,41 +193,37 @@
 
     def self_pair(leaf):
         x, y, z, m = load(leaf)
-        vb, q = features(x, y, z)
-        left = jnp.transpose(left_operand(vb, q)).astype(BF16)
+        two, _ = load_twice(leaf)
+        left = jnp.transpose(left_operand(two, x * x + y * y + z * z)).astype(BF16)
         turned[leaf] = left
-        high, rest = weights(left, right_operand(vb))
+        moment = force_operand(two, m)
+        moments[leaf] = moment
+        weight = weights(left, right_operand(features(two)))
         product = jnp.dot(
-            force_operand(vb, m), jnp.concatenate([high, rest], axis=0), preferred_element_type=F32
-        )
-        self_res[pl.ds(pl.multiple_of(leaf * 8, 8), 8), :] = finish(product, vb, m)
+            moment, jnp.concatenate(halves(weight), axis=0), preferred_element_type=F32
+        )
+        self_res[pl.ds(pl.multiple_of(leaf * 8, 8), 8), :] = finish(product, two, m)
 
     def listed_pair(p):
         target, source = pairs_s[0, 0, p], pairs_s[1, 0, p]
-        x, y, z, m_t = load(target)
-        vb_t, _ = features(x, y, z)
-        x, y, z, m_u = load(source)
-        vb_u, _ = features(x, y, z)
-        high, rest = weights(turned[target], right_operand(vb_u))
+        two, m = load_twice(source)
+        weight = weights(turned[target], right_operand(features(two)))
         onto_source = jnp.dot(
-            force_operand(vb_t, m_t), jnp.concatenate([high, rest], axis=0),
-            preferred_element_type=F32,
-        )
-        kept[p, :, :width] = high
-        kept[p, :, width:] = rest
-        src_res[pl.ds(pl.multiple_of(p * 8, 8), 8), :] = finish(onto_source, vb_u, m_u)
+            moments[target], jnp.concatenate(halves(weight), axis=0), preferred_element_type=F32
+        )
+        kept[p] = weight
+        src_res[pl.ds(pl.multiple_of(p * 8, 8), 8), :] = finish(onto_source, two, m)
 
     def target_side(p):
         target, source = pairs_s[0, 0, p], pairs_s[1, 0, p]
-        x, y, z, m_t = load(target)
-        vb_t, _ = features(x, y, z)
-        x, y, z, m_u = load(source)
-        vb_u, _ = features(x, y, z)
+        two_t, m_t = load_twice(target)
+        two_u, m_u = load_twice(source)
         onto_target = lax.dot_general(
-            force_operand(vb_u, m_u), kept[p], (((1,), (1,)), ((), ())),
+            force_operand(two_u, m_u), jnp.concatenate(halves(kept[p]), axis=1),
+            (((1,), (1,)), ((), ())),
             preferred_element_type=F32,
         )
-        tgt_res[pl.ds(pl.multiple_of(p * 8, 8), 8), :] = finish(onto_target, vb_t, m_t)
+        tgt_res[pl.ds(pl.multiple_of(p * 8, 8), 8), :] = finish(onto_target, two_t, m_t)
 
     def run(body, first, last, unroll=UNROLL):
         def step(i, carry):
@@ -286,6 +289,10 @@
             device_id=where, device_id_type=MESH,
         )
 
+    def centre(b, c):
+        source = ghost.at[OFFSETS.index((0, b)), part(c), :]
+        return give(source, slot_of(0, b), device[(0, b)], c, 1)
+
     for c in range(3):
         ghost_force = jnp.dot(onto_ghost, src_parts[c], preferred_element_type=F32)
         for k in range(8):
@@ -293,24 +300,33 @@
         for a in (-1, 1):
             for b in (-1, 1):
                 to_space, to_sub = device[(a, b)]
+                slot, group = slot_of(a, b), jnp.where(wraps[b], 1, 0)
+                if b < 0:
+                    slot, group = jnp.where(wraps[b], 8 + (a + 1) // 2, slot), 2 * group
+                    to_sub = jnp.where(wraps[b], r, to_sub)
                 give(
-                    ghost.at[OFFSETS.index((a, b)), part(c), :], slot_of(a, b),
-                    (jnp.where(wraps[b], to_space, s), to_sub), c, jnp.where(wraps[b], 1, 0),
+                    ghost.at[OFFSETS.index((a, b)), part(c), :], slot,
+                    (jnp.where(wraps[b], to_space, s), to_sub), c, group,
                 ).start()
-    for c in range(3):
-        for b in (-1, 1):
-            give(
-                ghost.at[OFFSETS.index((0, b)), part(c), :], slot_of(0, b), device[(0, b)], c, 1
-            ).start()
-
-    def took(c, last, at_edge, inside):
-        for which, count in ((edge, at_edge), (jnp.logical_not(edge), inside)):
-            @pl.when(which)
+
+        @pl.when(wraps[1])
+        def _():
+            centre(1, c).start()
+
+    for b in (-1, 1):
+        @pl.when(jnp.logical_not(wraps[b]))
+        def _():
+            for c in range(3):
+                centre(b, c).start()
+
+    def took(c, last, which, there, elsewhere):
+        for where, count in ((which, there), (jnp.logical_not(which), elsewhere)):
+            @pl.when(where)
             def _():
                 whole(came.at[c, pl.ds(0, count)], back_recv.at[last, c]).wait_recv()
 
     for c in range(3):
-        took(c, 0, 2, 4)
+        took(c, 0, edge, 2, 4)
 
         for a in (-1, 1):
             side = (a + 1) // 2
@@ -321,6 +337,16 @@
             )
             give(crossing.at[side, part(c), :], 6 + side, device[(a, 0)], c, 1).start()
     run(target_side, 0, pairs)
+
+    @pl.when(wraps[-1])
+    def _():
+        for c in range(3):
+            whole(came.at[c, pl.ds(8, 2)], back_recv.at[2, c]).wait_recv()
+            gathered[part(c), :] = (
+                ghost[OFFSETS.index((0, -1)), part(c), :] + came[c, 8] + came[c, 9]
+            )
+            give(gathered.at[part(c), :], slot_of(0, -1), device[(0, -1)], c, 1).start()
+
     tgt_all = jnp.concatenate([stacked(component(tgt_res, c, pairs)) for c in range(3)], axis=1)
     hit_t = onehot(leaves, 0, tgt_row, pair_live)
     hit_s = onehot(leaves, 0, src_row, pair_live)
@@ -335,11 +361,11 @@
         component(self_res, c, leaves) + own_force[:, c * width:(c + 1) * width] for c in range(3)
     ]
     for c in range(3):
-        took(c, 1, 6, 4)
-
-        far = [came[c, jnp.where(wraps[-1], slot_of(a, 1), slot_of(a, -1))] for a in (-1, 1)]
+        took(c, 1, wraps[-1], 6, 4)
+
+        far = [came[c, jnp.where(wraps[1], 4, slot_of(a, 1))] for a in (-1, 1)]
         returned = stacked(
-            came[c, 4] + came[c, 5] + came[c, 6] + came[c, 7] + jnp.where(edge, far[0] + far[1], 0.0)
+            came[c, 4] + came[c, 5] + came[c, 6] + came[c, 7] + jnp.where(wraps[-1], far[0] + far[1], 0.0)
         )
         out[c, 0] = own_force[c] + jnp.dot(onto_own, returned, preferred_element_type=F32)
     for which, sem, count in ((r == 0, 0, 6), (r != 0, 0, 8), (wraps[1], 2, 2)):
@@ -373,17 +399,19 @@
             pltpu.VMEM((4 * (leaves + 8 * sent), width), F32),
             pltpu.VMEM((4 * sent, width), F32),
             pltpu.VMEM((leaves, width, 48), BF16),
-            pltpu.VMEM((pairs, width, 2 * width), BF16),
+            pltpu.VMEM((leaves, 16, 2 * width), BF16),
+            pltpu.VMEM((pairs, width, width), F32),
             pltpu.VMEM((8 * leaves, width), F32),
             pltpu.VMEM((8 * pairs, width), F32),
             pltpu.VMEM((8 * pairs, width), F32),
             pltpu.VMEM((8, 3 * sent, width), F32),
-            pltpu.VMEM((3, 8, sent, width), F32),
+            pltpu.VMEM((3, 10, sent, width), F32),
             pltpu.VMEM((2, 3 * sent, width), F32),
+            pltpu.VMEM((3 * sent, width), F32),
             pltpu.SemaphoreType.DMA((10,)),
             pltpu.SemaphoreType.DMA((3,)),
             pltpu.SemaphoreType.DMA((2 * CHUNKS + 2,)),
-            pltpu.SemaphoreType.DMA((2, 3)),
+            pltpu.SemaphoreType.DMA((3, 3)),
         ],
         compiler_params=pltpu.CompilerParams(collective_id=0, has_side_effects=True),
     )(positions, masses, occupancy, export_slots, export_count, pair_list, pair_count)

time: 23.5 us -> 23 us (0.979)
  Pallas kernels: 21.4 us -> 20.9 us
    pallas_call x1, Pallas kernels: 21.4 us -> 20.9 us  [local(): pl.pallas_call(kernel, out_shape=pltpu.VMEM(positions.shape, F32), in_spe...]
where the time goes in v3:
time: 23 us; the launch traced here: 22.8 us
  Pallas kernels  20.9 us (91%)
  between operations  1.3 us (6%)
  local copies, waits for them, and re-layouts  0.64 us (3%)
    pallas_call x1, Pallas kernels, local(): pl.pallas_call(kernel, out_shape=pltpu.VMEM(positions.shape, F32), in_spe...  20.9 us
    unnamed x1, local copies, waits for them, and re-layouts  0.64 us

profile of v3, /device:TPU:0, one launch (start us, length us, event | category | flops | bytes accessed | tf_op | source)
XLA Modules:
  0.0 22.8 jit_solution(3372628619338645904)
XLA Ops:
  1.3 20.9 %shard_map.73 = f32[3,1,64,128]{3,2,1,0:T(8,128)S(1)} custom-call(f32[3,1,64,128]{3,2,1,0:T(8,128)} %pos_in.1, f32[1,64,128]{2,1,0:T(8,128)} %mass_in.1, s32[1,64]{1,0:T(1,128)} %occ_in.1, s32[1,32]{1,0:T(1,128)} %slots_in.1, s32[1,1]{1,0:T(1,128)S(6)} %copy.10.count_in, s32[2,1,64]{2,1,0:T(1,128)} %pairs_in.1, s32[1,1]{1,0:T(1,128)S(6)} %copy.11.live_in), custom_call_target="tpu_custom_call" | custom-call | tf_op jit(solution)/shard_map/pallas_call | solution.py:383
  22.2 0.6 %copy.9 = f32[3,1,64,128]{3,2,1,0:T(8,128)} copy(f32[3,1,64,128]{3,2,1,0:T(8,128)S(1)} %shard_map.73) | data formatting | bytes 196608
